TPU v7x, 256 devices: a whole 4x4x8 slice. The times are simulated.
256 devices in a mesh: replica: 64 (over z, y, core), model: 4 (over x).
Axes of the slice: x: 4, y: 4, z: 8, core: 2. Of those that a mesh axis runs over, the one named last changes fastest.
Arguments:
- slope_query: bfloat16 [64, 1024, 1024], P('replica', None, 'model'), may hold values from -8 to 8
- slope_key: bfloat16 [64, 1024, 1024], P('replica', None, 'model'), may hold values from -8 to 8
- slope_value: bfloat16 [64, 1024, 1024], P('replica', None, 'model'), may hold values from -8 to 8
- slope_mixed: bfloat16 [64, 1024, 1024], P('replica', 'model'), may hold values from -8 to 8
- slope_norm: bfloat16 [64, 1024], P('replica'), may hold values from -16 to 16
- param_query: float32 [1024, 1024], P('replica', 'model'), may hold values from -0.5 to 0.5
- param_key: float32 [1024, 1024], P('replica', 'model'), may hold values from -0.5 to 0.5
- param_value: float32 [1024, 1024], P('replica', 'model'), may hold values from -0.5 to 0.5
- param_mixed: float32 [1024, 1024], P('model', 'replica'), may hold values from -0.5 to 0.5
- param_norm: float32 [1024], P('replica'), may hold values from 0.25 to 1.75
- state_query: float32 [1024, 1024], P('replica', 'model'), may hold values from 0.0001953125 to 0.001953125
- state_key: float32 [1024, 1024], P('replica', 'model'), may hold values from 0.0001953125 to 0.001953125
- state_value: float32 [1024, 1024], P('replica', 'model'), may hold values from 0.0001953125 to 0.001953125
- state_mixed: float32 [1024, 1024], P('model', 'replica'), may hold values from 0.0001953125 to 0.001953125
- state_norm: float32 [1024], P('replica'), may hold values from 0.05 to 0.8
Outputs:
- half_query: bfloat16 [1024, 1024], P(None, 'model')
- half_key: bfloat16 [1024, 1024], P(None, 'model')
- half_value: bfloat16 [1024, 1024], P(None, 'model')
- half_mixed: bfloat16 [1024, 1024], P('model')
- half_norm: bfloat16 [1024], replicated
- next_query: float32 [1024, 1024], P('replica', 'model')
- next_key: float32 [1024, 1024], P('replica', 'model')
- next_value: float32 [1024, 1024], P('replica', 'model')
- next_mixed: float32 [1024, 1024], P('model', 'replica')
- next_norm: float32 [1024], P('replica')
- state_new_query: float32 [1024, 1024], P('replica', 'model')
- state_new_key: float32 [1024, 1024], P('replica', 'model')
- state_new_value: float32 [1024, 1024], P('replica', 'model')
- state_new_mixed: float32 [1024, 1024], P('model', 'replica')
- state_new_norm: float32 [1024], P('replica')
All inputs are finite; a program needn't handle non-finite values.
Results may differ from a plain program's by a relative error of at most 0.001.
Values may be sent and summed in bfloat16 or wider, within the bound.
No kernel may reach another device: no remote copies, remote signals or barrier semaphores. Data moves between devices by JAX's collectives and lax.ppermute only.
A program may use at most 64 MiB of HBM per device.

v0:
```python
import jax
import jax.numpy as jnp
from jax import lax
from jax.sharding import PartitionSpec as P

learn_rate = 0.025
hold_rate = 0.7


def in_blocks(value, dim, count):
    before, after = (value.shape[:dim], value.shape[dim + 1 :])
    return jnp.moveaxis(value.reshape(*before, count, -1, *after), dim, 0)


def sum_together(arrays, axis, dims):
    count = lax.axis_size(axis)
    blocks = [in_blocks(a, dim, count) for a, dim in zip(arrays, dims)]
    lines = jnp.concatenate([b.reshape(count, -1) for b in blocks], axis=1)
    rows = max(16, -(-lines.shape[1] // 1024) * 8)
    lines = jnp.pad(lines, ((0, 0), (0, rows * 128 - lines.shape[1]))).reshape(-1, 128)
    vector, at, gathered = (lax.psum_scatter(lines, axis, tiled=True).reshape(-1), 0, [])
    for b in blocks:
        part = b[0]
        gathered.append(vector[at : at + part.size].reshape(part.shape))
        at += part.size
    return tuple(gathered)


def sent_to_all(value, axis):
    copies = jnp.broadcast_to(value, (lax.axis_size(axis), *value.shape))
    return lax.all_to_all(copies, axis, split_axis=0, concat_axis=0, tiled=True)


def of_everyone(value, axis):
    everything = sent_to_all(value, axis)
    return jnp.sum(everything, axis=0)


def packed_total(arrays, axis):
    ends = [0]
    for a in arrays:
        ends.append(ends[-1] + a.size)
    total = of_everyone(jnp.concatenate([a.ravel() for a in arrays]), axis)
    return tuple((total[b:e].reshape(a.shape) for a, b, e in zip(arrays, ends, ends[1:])))


def turned_gather(arrays, axis, dims):
    turned = [jnp.moveaxis(a, dim, 0) for a, dim in zip(arrays, dims)]
    widths = [t[0].size for t in turned]
    both = jnp.concatenate([t.reshape(-1, w) for t, w in zip(turned, widths)], axis=1)
    result = lax.all_gather(both, axis, axis=0, tiled=True)
    blocks = jnp.split(result, [sum(widths[:k]) for k in range(1, len(widths))], axis=1)
    return tuple(
        (
            jnp.moveaxis(b.reshape(-1, *t.shape[1:]), 0, dim)
            for b, t, dim in zip(blocks, turned, dims)
        )
    )


def local(
    slope_query,
    slope_key,
    slope_value,
    slope_mixed,
    slope_norm,
    param_query,
    param_key,
    param_value,
    param_mixed,
    param_norm,
    state_query,
    state_key,
    state_value,
    state_mixed,
    state_norm,
):
    mean_query, mean_key, mean_value, mean_mixed, mean_norm = sum_together(
        (
            slope_query[0].astype(jnp.float32),
            slope_key[0].astype(jnp.float32),
            slope_value[0].astype(jnp.float32),
            slope_mixed[0].astype(jnp.float32),
            slope_norm[0].astype(jnp.float32),
        ),
        "replica",
        (0, 0, 0, 1, 0),
    )
    mean_rate = lax.axis_size("replica") ** (-0.5)
    mean_query = mean_query * mean_rate
    mean_key = mean_key * mean_rate
    mean_value = mean_value * mean_rate
    mean_mixed = mean_mixed * mean_rate
    mean_norm = mean_norm * mean_rate
    (
        own_query,
        own_key,
        own_value,
        own_mixed,
        slope_query_norm,
        slope_key_norm,
        slope_value_norm,
        slope_mixed_norm,
    ) = packed_total(
        (
            jnp.sum(param_query * param_query, axis=1, keepdims=True),
            jnp.sum(param_key * param_key, axis=1, keepdims=True),
            jnp.sum(param_value * param_value, axis=1, keepdims=True),
            jnp.sum(param_mixed * param_mixed, axis=0, keepdims=True),
            jnp.sum(mean_query * mean_query, axis=1, keepdims=True),
            jnp.sum(mean_key * mean_key, axis=1, keepdims=True),
            jnp.sum(mean_value * mean_value, axis=1, keepdims=True),
            jnp.sum(mean_mixed * mean_mixed, axis=0, keepdims=True),
        ),
        "model",
    )
    mean_query = mean_query * (jnp.sqrt(own_query) * lax.rsqrt(slope_query_norm + 1e-06))
    mean_key = mean_key * (jnp.sqrt(own_key) * lax.rsqrt(slope_key_norm + 1e-06))
    mean_value = mean_value * (jnp.sqrt(own_value) * lax.rsqrt(slope_value_norm + 1e-06))
    mean_mixed = mean_mixed * (jnp.sqrt(own_mixed) * lax.rsqrt(slope_mixed_norm + 1e-06))
    state_new_query = hold_rate * state_query + (1.0 - hold_rate) * mean_query * mean_query
    next_query = param_query - learn_rate * mean_query * lax.rsqrt(state_new_query + 1e-06)
    state_new_key = hold_rate * state_key + (1.0 - hold_rate) * mean_key * mean_key
    next_key = param_key - learn_rate * mean_key * lax.rsqrt(state_new_key + 1e-06)
    state_new_value = hold_rate * state_value + (1.0 - hold_rate) * mean_value * mean_value
    next_value = param_value - learn_rate * mean_value * lax.rsqrt(state_new_value + 1e-06)
    state_new_mixed = hold_rate * state_mixed + (1.0 - hold_rate) * mean_mixed * mean_mixed
    next_mixed = param_mixed - learn_rate * mean_mixed * lax.rsqrt(state_new_mixed + 1e-06)
    state_new_norm = hold_rate * state_norm + (1.0 - hold_rate) * mean_norm * mean_norm
    next_norm = param_norm - learn_rate * mean_norm * lax.rsqrt(state_new_norm + 1e-06)
    half_query, half_key, half_value, half_mixed, half_norm = turned_gather(
        (
            next_query.astype(jnp.bfloat16),
            next_key.astype(jnp.bfloat16),
            next_value.astype(jnp.bfloat16),
            next_mixed.astype(jnp.bfloat16),
            next_norm.astype(jnp.bfloat16),
        ),
        "replica",
        (0, 0, 0, 1, 0),
    )
    return (
        half_query,
        half_key,
        half_value,
        half_mixed,
        half_norm,
        next_query,
        next_key,
        next_value,
        next_mixed,
        next_norm,
        state_new_query,
        state_new_key,
        state_new_value,
        state_new_mixed,
        state_new_norm,
    )


def solution(mesh):
    return jax.shard_map(
        local,
        mesh=mesh,
        in_specs=(
            P("replica", None, "model"),
            P("replica", None, "model"),
            P("replica", None, "model"),
            P("replica", "model", None),
            P("replica", None),
            P("replica", "model"),
            P("replica", "model"),
            P("replica", "model"),
            P("model", "replica"),
            P("replica"),
            P("replica", "model"),
            P("replica", "model"),
            P("replica", "model"),
            P("model", "replica"),
            P("replica"),
        ),
        out_specs=(
            P(None, "model"),
            P(None, "model"),
            P(None, "model"),
            P("model", None),
            P(),
            P("replica", "model"),
            P("replica", "model"),
            P("replica", "model"),
            P("model", "replica"),
            P("replica"),
            P("replica", "model"),
            P("replica", "model"),
            P("replica", "model"),
            P("model", "replica"),
            P("replica"),
        ),
        check_vma=False,
    )
```

profile of v0, /device:TPU:1, one launch (start us, length us, event | category | flops | bytes accessed | tf_op | source)
XLA Modules:
  0.0 329.9 jit_solution(10158640224522271844)
XLA Ops:
  7.2 1.3 convert_element_type.42
  8.6 1.0 convert_element_type.43
  9.7 2.1 convert_element_type.44
  11.8 1.0 copy.76
  12.8 2.6 copy.77
  15.4 1.1 copy.78
  16.6 1.1 constant_dynamic-update-slice_fusion.3
  17.8 1.1 constant_dynamic-update-slice_fusion.2
  18.9 2.4 pad_convert_fusion
  21.3 5.0 %reshape.132 = f32[8704,128]{1,0:T(8,128)} reshape(f32[64,17408]{1,0:T(8,128)} %pad_convert_fusion) | data formatting | bytes 8912896 | tf_op jit(solution)/shard_map/reshape | solution.py:20
  26.5 0.6 copy-done.15
  27.0 0.6 dynamic-slice
  28.5 0.1 multiply_reduce_fusion.5
  28.6 196.8 %all-reduce.4.cloned.1.call-done = f32[8704,128]{1,0:T(8,128)} async-done(((f32[8704,128]{1,0:T(8,128)}), f32[8704,128]{1,0:T(8,128)}) %all-reduce.4.cloned.1.call-update) | async-done | bytes 4456464
  225.4 1.0 multiply_reduce_fusion.1
  226.6 0.1 reduce_sum.108
  226.7 0.1 reduce_sum.111
  226.9 0.1 reduce_sum.114
  227.3 0.6 broadcast_in_dim.3
  227.8 4.0 %all-to-all-start = ((f32[4,1,128]{2,1,0:T(1,128)}), f32[4,1,128]{2,1,0:T(1,128)S(1)}, u32[]{:S(2)}, u32[]{:S(2)}) async-start(f32[4,1,128]{2,1,0:T(1,128)} %broadcast_in_dim.3), calls=%async_computation | async-start | bytes 4096 | tf_op jit(solution)/shard_map/all_to_all | solution.py:31
  231.8 0.9 dynamic-slice_bitcast_fusion
  232.7 0.5 convert_bitcast_fusion
  233.4 2.4 all-to-all-done
  236.0 0.7 constant_dynamic-update-slice_fusion.9
  236.7 0.7 constant_dynamic-update-slice_fusion.8
  237.4 0.7 constant_dynamic-update-slice_fusion.7
  238.1 0.7 constant_dynamic-update-slice_fusion.6
  238.8 0.6 copy-done.7
  239.4 78.3 %all-gather.2.cloned.1.call-done = bf16[1024,1025]{1,0:T(8,128)(2,1)} async-done(((bf16[16,1025]{1,0:T(8,128)(2,1)}), bf16[1024,1025]{1,0:T(8,128)(2,1)}) %all-gather.2.cloned.1.call-update) | async-done | bytes 2099216 | tf_op jit(solution)/shard_map/all_gather | solution.py:51
  317.7 2.7 slice_bitcast_fusion
  320.4 1.0 copy.82
  321.4 1.7 slice_reduce_fusion
  (55 shorter events, 1.3 us)
Async XLA Ops:
  7.2 1.4 copy-start.1
  7.2 218.2 %all-reduce.4.cloned.1.call-start = ((), (), s32[]{:S(2)}) async-start(), calls=%async_computation.2 | async-start | bytes 8912896
  8.6 3.1 copy-start.2
  11.7 4.8 %copy-start.12 = (bf16[1,1024]{1,0:T(2,128)(2,1)S(1)}, bf16[1,1024]{1,0:T(2,128)(2,1)}, u32[]{:S(2)}) copy-start(bf16[1,1024]{1,0:T(2,128)(2,1)} %param.19) | copy-start | bytes 6148
  16.5 2.3 copy-start
  26.3 0.7 copy-start.15
  26.4 1.9 copy-start.3
  26.4 2.0 copy-start.6
  26.4 2.2 copy-start.4
  26.4 2.2 copy-start.5
  26.4 206.3 %copy-start.13 = (f32[16]{0:T(128)S(1)}, f32[16]{0:T(128)}, u32[]{:S(2)}) copy-start(f32[16]{0:T(128)} %param.24) | copy-start | bytes 196
  26.4 206.3 %copy-start.14 = (f32[16]{0:T(128)S(1)}, f32[16]{0:T(128)}, u32[]{:S(2)}) copy-start(f32[16]{0:T(128)} %param.29) | copy-start | bytes 196
  26.4 209.6 %copy-start.8 = (f32[16,256]{1,0:T(8,128)S(1)}, f32[16,256]{1,0:T(8,128)}, u32[]{:S(2)}) copy-start(f32[16,256]{1,0:T(8,128)} %param.25) | copy-start | bytes 49156
  26.4 210.3 %copy-start.9 = (f32[16,256]{1,0:T(8,128)S(1)}, f32[16,256]{1,0:T(8,128)}, u32[]{:S(2)}) copy-start(f32[16,256]{1,0:T(8,128)} %param.26) | copy-start | bytes 49156
  26.4 211.0 %copy-start.10 = (f32[16,256]{1,0:T(8,128)S(1)}, f32[16,256]{1,0:T(8,128)}, u32[]{:S(2)}) copy-start(f32[16,256]{1,0:T(8,128)} %param.27) | copy-start | bytes 49156
  26.4 211.6 %copy-start.11 = (f32[256,16]{0,1:T(8,128)S(1)}, f32[256,16]{0,1:T(8,128)}, u32[]{:S(2)}) copy-start(f32[256,16]{0,1:T(8,128)} %param.28) | copy-start | bytes 49156
  227.8 8.0 %all-to-all-start = ((f32[4,1,128]{2,1,0:T(1,128)}), f32[4,1,128]{2,1,0:T(1,128)S(1)}, u32[]{:S(2)}, u32[]{:S(2)}) async-start(f32[4,1,128]{2,1,0:T(1,128)} %broadcast_in_dim.3), calls=%async_computation | async-start | bytes 4096 | tf_op jit(solution)/shard_map/all_to_all | solution.py:31
  231.8 85.9 %all-gather.2.cloned.1.call-start = ((), (), s32[]{:S(2)}) async-start(), calls=%async_computation.1 | async-start | bytes 2396160 | tf_op jit(solution)/shard_map/all_gather | solution.py:51
  238.8 0.6 copy-start.7
Sparse Core Ops, SparseCore 0:
  26.6 198.7 all-reduce.3
  239.5 78.1 all-gather.1
where the time goes:
time: 331 us; the launch traced here: 330 us
  waiting for transfers between devices  278 us (84%)
  local copies, waits for them, and re-layouts  25.9 us (8%)
  between operations  14.9 us (5%)
  other arithmetic  7.53 us (2%)
  starting transfers between devices  4.01 us (1%)
    unnamed x3, waiting for transfers between devices  197 us
    all_gather x1, waiting for transfers between devices, turned_gather(): result = lax.all_gather(both, axis, axis=0, tiled=True)  78.3 us
  transfers between devices with their start and end apart: 3, of which 3 were waited for; matrix products, arithmetic and copies ran while one was open for 1% of the time, Pallas kernels for 0%

commit v1 on v0

--- a/solution.py
+++ b/solution.py
@@ -48,7 +48,10 @@
     turned = [jnp.moveaxis(a, dim, 0) for a, dim in zip(arrays, dims)]
     widths = [t[0].size for t in turned]
     both = jnp.concatenate([t.reshape(-1, w) for t, w in zip(turned, widths)], axis=1)
-    result = lax.all_gather(both, axis, axis=0, tiled=True)
+    size = lax.axis_size(axis)
+    pieces = jnp.stack([both for _ in range(size)])
+    pieces = lax.all_to_all(pieces, axis, split_axis=0, concat_axis=0)
+    result = jnp.concatenate(pieces, axis=0)
     blocks = jnp.split(result, [sum(widths[:k]) for k in range(1, len(widths))], axis=1)
     return tuple(
         (

time: 331 us -> 319 us (0.964)
  waiting for transfers between devices: 278 us -> 199 us
  blocking collectives: 0 us -> 69.4 us
    all_gather x1 -> x0, waiting for transfers between devices: 78.3 us -> none  [turned_gather(): result = lax.all_gather(both, axis, axis=0, tiled=True)]
    all_to_all x0 -> x1, blocking collectives: none -> 69.4 us  [turned_gather(): pieces = lax.all_to_all(pieces, axis, split_axis=0, concat_axis=0)]
    unnamed x3 -> x2, waiting for transfers between devices: 197 us -> 197 us
  transfers between devices with their start and end apart: 3 -> 2, of which waited for: 3 -> 2; matrix products, arithmetic and copies ran while one was open for 1% -> 1% of each run, Pallas kernels for 0% -> 0%
where the time goes in v1:
time: 319 us; the launch traced here: 318 us
  waiting for transfers between devices  199 us (62%)
  blocking collectives  69.4 us (22%)
  local copies, waits for them, and re-layouts  23 us (7%)
  between operations  14.9 us (5%)
  other arithmetic  7.53 us (2%)
  starting transfers between devices  4.01 us (1%)
    unnamed x2, waiting for transfers between devices  197 us
    all_to_all x1, blocking collectives, turned_gather(): pieces = lax.all_to_all(pieces, axis, split_axis=0, concat_axis=0)  69.4 us
  transfers between devices with their start and end apart: 2, of which 2 were waited for; matrix products, arithmetic and copies ran while one was open for 1% of the time, Pallas kernels for 0%

profile of v1, /device:TPU:1, one launch (start us, length us, event | category | flops | bytes accessed | tf_op | source)
XLA Modules:
  0.0 318.1 jit_solution(17220949708572399076)
XLA Ops:
  7.2 1.3 convert_element_type.42
  8.6 1.0 convert_element_type.43
  9.7 2.1 convert_element_type.44
  11.8 1.0 copy.78
  12.8 2.6 copy.79
  15.4 1.1 copy.80
  16.6 1.1 constant_dynamic-update-slice_fusion.3
  17.8 1.1 constant_dynamic-update-slice_fusion.2
  18.9 2.4 pad_convert_fusion
  21.3 5.0 %reshape.138 = f32[8704,128]{1,0:T(8,128)} reshape(f32[64,17408]{1,0:T(8,128)} %pad_convert_fusion) | data formatting | bytes 8912896 | tf_op jit(solution)/shard_map/reshape | solution.py:20
  26.5 0.6 copy-done.14
  27.0 0.6 dynamic-slice
  28.5 0.1 multiply_reduce_fusion.5
  28.6 196.8 %all-reduce.4.cloned.1.call-done = f32[8704,128]{1,0:T(8,128)} async-done(((f32[8704,128]{1,0:T(8,128)}), f32[8704,128]{1,0:T(8,128)}) %all-reduce.4.cloned.1.call-update) | async-done | bytes 4456464
  225.4 1.0 multiply_reduce_fusion.1
  226.6 0.1 reduce_sum.108
  226.7 0.1 reduce_sum.111
  226.9 0.1 reduce_sum.114
  227.3 0.6 broadcast_in_dim.3
  227.8 4.0 %all-to-all-start = ((f32[4,1,128]{2,1,0:T(1,128)}), f32[4,1,128]{2,1,0:T(1,128)S(1)}, u32[]{:S(2)}, u32[]{:S(2)}) async-start(f32[4,1,128]{2,1,0:T(1,128)} %broadcast_in_dim.3), calls=%async_computation | async-start | bytes 4096 | tf_op jit(solution)/shard_map/all_to_all | solution.py:31
  231.8 0.9 dynamic-slice_bitcast_fusion
  232.7 0.5 convert_bitcast_fusion
  233.4 2.4 all-to-all-done
  236.0 0.7 constant_dynamic-update-slice_fusion.9
  236.7 0.7 constant_dynamic-update-slice_fusion.8
  237.4 0.7 constant_dynamic-update-slice_fusion.7
  238.1 0.7 constant_dynamic-update-slice_fusion.6
  238.8 0.2 stack.2
  239.0 69.4 %all_to_all.11 = bf16[64,16,1025]{2,1,0:T(8,128)(2,1)S(1)} all-to-all(bf16[64,16,1025]{2,1,0:T(8,128)(2,1)S(1)} %stack.2), channel_id=1, replica_groups=mesh['replica'=64,'model'=4] {'replica'}, dimensions={0} | all-to-all | bytes 4198400 | tf_op jit(solution)/shard_map/all_to_all | solution.py:53
  308.4 1.2 slice_bitcast_fusion
  309.5 0.7 slice_reduce_fusion
  310.3 1.0 copy.84
  (52 shorter events, 1.3 us)
Async XLA Ops:
  7.2 1.4 copy-start.1
  7.2 218.2 %all-reduce.4.cloned.1.call-start = ((), (), s32[]{:S(2)}) async-start(), calls=%async_computation.2 | async-start | bytes 8912896
  8.6 3.1 copy-start.2
  11.7 4.8 %copy-start.11 = (bf16[1,1024]{1,0:T(2,128)(2,1)S(1)}, bf16[1,1024]{1,0:T(2,128)(2,1)}, u32[]{:S(2)}) copy-start(bf16[1,1024]{1,0:T(2,128)(2,1)} %param.19) | copy-start | bytes 6148
  16.5 2.3 copy-start
  26.3 0.7 copy-start.14
  26.4 1.9 copy-start.3
  26.4 2.0 copy-start.6
  26.4 2.2 copy-start.4
  26.4 2.2 copy-start.5
  26.4 206.3 %copy-start.12 = (f32[16]{0:T(128)S(1)}, f32[16]{0:T(128)}, u32[]{:S(2)}) copy-start(f32[16]{0:T(128)} %param.24) | copy-start | bytes 196
  26.4 206.3 %copy-start.13 = (f32[16]{0:T(128)S(1)}, f32[16]{0:T(128)}, u32[]{:S(2)}) copy-start(f32[16]{0:T(128)} %param.29) | copy-start | bytes 196
  26.4 209.6 %copy-start.7 = (f32[16,256]{1,0:T(8,128)S(1)}, f32[16,256]{1,0:T(8,128)}, u32[]{:S(2)}) copy-start(f32[16,256]{1,0:T(8,128)} %param.25) | copy-start | bytes 49156
  26.4 210.3 %copy-start.8 = (f32[16,256]{1,0:T(8,128)S(1)}, f32[16,256]{1,0:T(8,128)}, u32[]{:S(2)}) copy-start(f32[16,256]{1,0:T(8,128)} %param.26) | copy-start | bytes 49156
  26.4 211.0 %copy-start.9 = (f32[16,256]{1,0:T(8,128)S(1)}, f32[16,256]{1,0:T(8,128)}, u32[]{:S(2)}) copy-start(f32[16,256]{1,0:T(8,128)} %param.27) | copy-start | bytes 49156
  26.4 211.6 %copy-start.10 = (f32[256,16]{0,1:T(8,128)S(1)}, f32[256,16]{0,1:T(8,128)}, u32[]{:S(2)}) copy-start(f32[256,16]{0,1:T(8,128)} %param.28) | copy-start | bytes 49156
  227.8 8.0 %all-to-all-start = ((f32[4,1,128]{2,1,0:T(1,128)}), f32[4,1,128]{2,1,0:T(1,128)S(1)}, u32[]{:S(2)}, u32[]{:S(2)}) async-start(f32[4,1,128]{2,1,0:T(1,128)} %broadcast_in_dim.3), calls=%async_computation | async-start | bytes 4096 | tf_op jit(solution)/shard_map/all_to_all | solution.py:31
Sparse Core Ops, SparseCore 0:
  26.6 198.7 all-reduce.3
